TPU v7x, 32 devices: a whole 2x2x4 slice. The times are simulated.
32 devices in a mesh: aa: 4 (over x, core), ba: 4 (over z), col: 2 (over y).
Axes of the slice: x: 2, y: 2, z: 4, core: 2. Of those that a mesh axis runs over, the one named last changes fastest.
Arguments:
- tokens: bfloat16 [64, 32, 64, 1024], P('aa', 'ba', 'col'), may hold values from -6 to 6
- norm_gain: float32 [1024], replicated, may hold values from 0.1 to 1.9
- in_weight: bfloat16 [1024, 3072], replicated, may hold values from -0.1875 to 0.1875
- skip_gain: float32 [1024], replicated, may hold values from 0.5 to 1.5
- spectrum_filter: bfloat16 [2, 64, 32, 64, 1024], P(None, ('ba', 'col'), None, None, 'aa'), may hold values from -4 to 4
- out_weight: bfloat16 [1024, 1024], replicated, may hold values from -0.1875 to 0.1875
Outputs:
- layer_out: bfloat16 [64, 32, 64, 1024], P('aa', 'ba', 'col')
All inputs are finite; a program needn't handle non-finite values.
Results may differ from a plain program's by a relative error of at most 0.014.
Values may be sent and summed in bfloat16 or wider, within the bound.
No kernel may reach another device: no remote copies, remote signals or barrier semaphores. Data moves between devices by JAX's collectives and lax.ppermute only.
A program may use at most 256 MiB of HBM per device.

v0:
```python
import math

import jax
import jax.numpy as jnp
from jax import lax
from jax.sharding import PartitionSpec as P

LA = 64
LB = 32
LC = 64
D = 1024


EPSILON = 1e-06


def dft_tables(length):
    counter = jnp.arange(length, dtype=jnp.int32)
    product = counter[:, None] * counter[None, :] % length
    angle = 2.0 * math.pi / length * product.astype(jnp.float32)
    factor = 1.0 / math.sqrt(length)
    return (
        (jnp.cos(angle) * factor).astype(jnp.bfloat16),
        (jnp.sin(angle) * factor).astype(jnp.bfloat16),
    )


def phase_pair(integer_phase, modulus):
    angle = 2.0 * math.pi / modulus * (integer_phase % modulus).astype(jnp.float32)
    return (jnp.cos(angle), jnp.sin(angle))


def contract(form, table, operand):
    return jnp.einsum(form, table, operand, preferred_element_type=jnp.float32)


def local(tokens, norm_gain, in_weight, skip_gain, spectrum_filter, out_weight):
    count_aa = lax.axis_size("aa")
    count_ba = lax.axis_size("ba")
    count_col = lax.axis_size("col")
    rows_i = LA // count_aa
    rows_j = LB // count_ba
    rows_k = LC // count_col
    blocks = count_ba * count_col
    freq_local = LA // blocks
    channels = D // count_aa
    points = LA * LB * LC
    flat = tokens.reshape(-1, D).astype(jnp.float32)
    meansq = jnp.mean(flat * flat, axis=-1, keepdims=True)
    normed = (flat * lax.rsqrt(meansq + EPSILON) * norm_gain).astype(jnp.bfloat16)
    projected = jnp.dot(normed, in_weight, preferred_element_type=jnp.float32)
    mixed = (projected[:, :D] * projected[:, 2 * D :]).astype(jnp.bfloat16)
    gate = projected[:, D : 2 * D].astype(jnp.bfloat16)
    local_block = mixed.reshape(rows_i, rows_j, rows_k, D)
    by_rows = lax.all_to_all(local_block, "aa", split_axis=3, concat_axis=0, tiled=True)
    cos_a, sin_a = dft_tables(LA)
    real_part = contract("fi,ijkx->fjkx", cos_a, by_rows)
    imag_part = -contract("fi,ijkx->fjkx", sin_a, by_rows)
    j_global = lax.axis_index("ba") * rows_j + jnp.arange(rows_j, dtype=jnp.int32)
    k_global = lax.axis_index("col") * rows_k + jnp.arange(rows_k, dtype=jnp.int32)
    freq_all = jnp.arange(LA, dtype=jnp.int32)
    cos_phi, sin_phi = phase_pair(
        (LC * j_global[None, :, None] + k_global[None, None, :]) * freq_all[:, None, None], points
    )
    cos_phi = cos_phi[..., None]
    sin_phi = sin_phi[..., None]
    first = jnp.stack(
        [real_part * cos_phi + imag_part * sin_phi, imag_part * cos_phi - real_part * sin_phi]
    ).astype(jnp.bfloat16)
    shaped = first.reshape(2, blocks, 1, freq_local, rows_j, rows_k, channels)
    moved = lax.all_to_all(shaped, ("ba", "col"), split_axis=1, concat_axis=2, tiled=True)
    moved = moved.reshape(2, count_ba, count_col, freq_local, rows_j, rows_k, channels)
    cos_b, sin_b = dft_tables(LB)
    cos_b = cos_b.reshape(LB, count_ba, rows_j)
    sin_b = sin_b.reshape(LB, count_ba, rows_j)
    moved_real = moved[0]
    moved_imag = moved[1]
    form_two = "gbj,bcfjkx->fgckx"
    real_part = contract(form_two, cos_b, moved_real) + contract(form_two, sin_b, moved_imag)
    imag_part = contract(form_two, cos_b, moved_imag) - contract(form_two, sin_b, moved_real)
    index_g = jnp.arange(LB, dtype=jnp.int32)
    index_k = jnp.arange(LC, dtype=jnp.int32)
    cos_psi, sin_psi = phase_pair(index_g[:, None] * index_k[None, :], LB * LC)
    cos_psi = cos_psi.reshape(1, LB, count_col, rows_k, 1)
    sin_psi = sin_psi.reshape(1, LB, count_col, rows_k, 1)
    second_real = (real_part * cos_psi + imag_part * sin_psi).astype(jnp.bfloat16)
    second_imag = (imag_part * cos_psi - real_part * sin_psi).astype(jnp.bfloat16)
    cos_c, sin_c = dft_tables(LC)
    cos_c = cos_c.reshape(LC, count_col, rows_k)
    sin_c = sin_c.reshape(LC, count_col, rows_k)
    form_three = "hck,fgckx->fghx"
    spec_real = contract(form_three, cos_c, second_real) + contract(form_three, sin_c, second_imag)
    spec_imag = contract(form_three, cos_c, second_imag) - contract(form_three, sin_c, second_real)
    filt_real = spectrum_filter[0].astype(jnp.float32)
    filt_imag = spectrum_filter[1].astype(jnp.float32)
    filtered_real = (filt_real * spec_real - filt_imag * spec_imag).astype(jnp.bfloat16)
    filtered_imag = (filt_real * spec_imag + filt_imag * spec_real).astype(jnp.bfloat16)
    form_back_three = "hck,fghx->fgckx"
    real_part = contract(form_back_three, cos_c, filtered_real) - contract(
        form_back_three, sin_c, filtered_imag
    )
    imag_part = contract(form_back_three, cos_c, filtered_imag) + contract(
        form_back_three, sin_c, filtered_real
    )
    third_real = (real_part * cos_psi - imag_part * sin_psi).astype(jnp.bfloat16)
    third_imag = (imag_part * cos_psi + real_part * sin_psi).astype(jnp.bfloat16)
    form_back_two = "gbj,fgckx->bcfjkx"
    real_part = contract(form_back_two, cos_b, third_real) - contract(
        form_back_two, sin_b, third_imag
    )
    imag_part = contract(form_back_two, cos_b, third_imag) + contract(
        form_back_two, sin_b, third_real
    )
    slot = lax.axis_index("ba") * count_col + lax.axis_index("col")
    freq_global = slot * freq_local + jnp.arange(freq_local, dtype=jnp.int32)
    j_all = jnp.arange(LB, dtype=jnp.int32).reshape(count_ba, rows_j)
    k_all = jnp.arange(LC, dtype=jnp.int32).reshape(count_col, rows_k)
    integer_phase = (
        LC * j_all[:, None, None, :, None] + k_all[None, :, None, None, :]
    ) * freq_global[None, None, :, None, None]
    cos_back, sin_back = phase_pair(integer_phase, points)
    cos_back = cos_back[..., None]
    sin_back = sin_back[..., None]
    back_second = jnp.stack(
        [real_part * cos_back - imag_part * sin_back, imag_part * cos_back + real_part * sin_back]
    ).astype(jnp.bfloat16)
    shaped = back_second.reshape(2, 1, blocks, freq_local, rows_j, rows_k, channels)
    returned = lax.all_to_all(shaped, ("ba", "col"), split_axis=2, concat_axis=1, tiled=True)
    returned = returned.reshape(2, LA, rows_j, rows_k, channels)
    conv_part = (
        contract("fi,fjkx->ijkx", cos_a, returned[0])
        - contract("fi,fjkx->ijkx", sin_a, returned[1])
    ).astype(jnp.bfloat16)
    conv_tokens = lax.all_to_all(conv_part, "aa", split_axis=0, concat_axis=3, tiled=True)
    conv_flat = conv_tokens.reshape(-1, D).astype(jnp.float32)
    gated = (gate.astype(jnp.float32) * (conv_flat + skip_gain * mixed.astype(jnp.float32))).astype(
        jnp.bfloat16
    )
    layer_out = jnp.dot(gated, out_weight, preferred_element_type=jnp.float32).astype(jnp.bfloat16)
    return layer_out.reshape(rows_i, rows_j, rows_k, D)


def solution(mesh):
    in_specs = (
        P("aa", "ba", "col", None),
        P(),
        P(),
        P(),
        P(None, ("ba", "col"), None, None, "aa"),
        P(),
    )
    out_specs = P("aa", "ba", "col", None)
    return jax.shard_map(local, mesh=mesh, in_specs=in_specs, out_specs=out_specs, check_vma=False)
```

profile of v0, /device:TPU:0, one launch (start us, length us, event | category | flops | bytes accessed | tf_op | source)
XLA Modules:
  0.0 1626.5 jit_solution(17985871560991421885)
XLA Ops:
  10.8 31.4 %fusion.236 = f32[4096,3072]{1,0:T(8,128)} fusion(bf16[4096,1024]{1,0:T(8,128)(2,1)S(1)} %fusion.14, bf16[1024,3072]{1,0:T(8,128)(2,1)S(1)} %copy-done.8), kind=kOutput, calls=%fused_computation.280 | convolution fusion | flops 25769803776 | bytes 65011712 | tf_op jit(solution)/shard_map/dot_general | solution.py:51
  42.2 15.1 fusion.4
  57.4 44.2 %copy.74 = bf16[16,8,32,1024]{2,1,0,3:T(8,128)(2,1)} copy(bf16[16,8,32,1024]{3,2,1,0:T(8,128)(2,1)} %bitcast.244) | data formatting | bytes 16777216 | tf_op jit(solution)/shard_map/reshape | solution.py:54
  101.6 50.4 %reshape.452 = bf16[4,2,524288]{2,1,0:T(2,128)(2,1)} reshape(bf16[1024,16,8,32]{3,2,1,0:T(8,128)(2,1)} %bitcast.236) | data formatting | bytes 16777216
  159.5 92.4 %all-to-all-done = bf16[4,2,524288]{2,1,0:T(2,128)(2,1)} async-done(((bf16[4,2,524288]{2,1,0:T(2,128)(2,1)}), bf16[4,2,524288]{2,1,0:T(2,128)(2,1)}, u32[]{:S(2)}, u32[]{:S(2)}) %all-to-all-start) | async-done | bytes 8388640 | tf_op jit(solution)/shard_map/all_to_all | solution.py:55
  251.9 37.0 %reshape.453 = bf16[1024,16,8,32]{3,2,1,0:T(8,128)(2,1)} reshape(bf16[4,2,524288]{2,1,0:T(2,128)(2,1)} %all-to-all-done) | data formatting | bytes 16777216
  288.9 45.4 %copy.75 = bf16[16,8,32,4,256]{4,0,3,2,1:T(8,128)(2,1)} copy(bf16[16,8,32,4,256]{2,1,0,4,3:T(8,128)(2,1)} %bitcast.235) | data formatting | bytes 16777216 | tf_op jit(solution)/shard_map/all_to_all | solution.py:55
  399.1 358.3 %all-to-all-done.1 = bf16[2,8,1,8,8,32,256]{6,5,4,3,2,0,1:T(8,128)(2,1)} async-done(((bf16[2,8,1,8,8,32,256]{6,5,4,3,2,0,1:T(8,128)(2,1)}), bf16[2,8,1,8,8,32,256]{6,5,4,3,2,0,1:T(8,128)(2,1)}, u32[]{:S(2)}, u32[]{:S(2)}) %all-to-all-start.1) | async-done | bytes 16777248 | tf_op jit(solution)/shard_map/all_to_all | solution.py:71
  767.8 17.5 %fusion.45 = f32[2,8,32,256,32,1]{3,4,5,2,1,0:T(8,128)} fusion(bf16[4,2,8,8,32,256]{5,4,3,2,1,0:T(8,128)(2,1)} %bitcast.241, s32[4,8]{1,0:T(4,128)S(1)} %multiply_add_fusion), kind=kOutput, calls=%fused_computation.77 | convolution fusion | flops 268451840 | bytes 25165952 | tf_op jit(solution)/shard_map/gbj,bcfjkx->fgckx/dot_general | solution.py:34
  785.3 14.3 fusion.47
  808.5 26.6 %fusion.10 = (bf16[8,32,2,32,256]{4,1,3,0,2:T(8,128)(2,1)}, bf16[8,32,2,32,256]{4,1,3,0,2:T(8,128)(2,1)}) fusion(f32[32,2,32]{0,2,1:T(8,128)S(1)} %get-tuple-element.24, f32[32,2,32]{0,2,1:T(8,128)S(1)} %get-tuple-element.23, f32[2,8,32,256,32,1]{3,4,5,2,1,0:T(8,128)} %fusion.47, f32[2,8,32,256,32,1]{3,4,5,2,1,0:T(8,128)} %fusion.45, ...), kind=kOutput, calls=%fused_computation.26 | convolution fusion | flops 310394880 | bytes 75513984 | tf_op jit(solution)/shard_map/gbj,bcfjkx->fgckx/dot_general | solution.py:34
  835.2 16.0 fusion.35
  863.5 21.3 %bitcast_subtract_fusion = f32[8,32,256,64]{2,3,1,0:T(8,128)} fusion(f32[8,32,256,64,1]{2,3,4,1,0:T(8,128)} %fusion.35, bf16[8,32,2,32,256]{4,1,3,0,2:T(8,128)(2,1)} %get-tuple-element.5, s32[2,32]{1,0:T(2,128)S(1)} %multiply_add_fusion.1), kind=kOutput, calls=%fused_computation.21 | convolution fusion | flops 541130752 | bytes 41943296 | tf_op jit(solution)/shard_map/hck,fgckx->fghx/dot_general | solution.py:34
  884.8 24.5 %fusion.20 = (bf16[8,32,64,256,1]{3,2,4,1,0:T(8,128)(2,1)}, bf16[8,32,64,256,1]{3,2,4,1,0:T(8,128)(2,1)S(1)}) fusion(f32[8,32,256,64]{2,3,1,0:T(8,128)} %bitcast_subtract_fusion, bf16[2,8,32,64,256]{4,3,2,1,0:T(8,128)(2,1)} %param.10, s32[2,32]{1,0:T(2,128)S(1)} %multiply_add_fusion.1, bf16[8,32,2,32,256]{4,1,3,0,2:T(8,128)(2,1)} %get-tuple-element.6, ...), kind=kOutput, calls=%fused_computation.52 | convolution fusion | flops 583073792 | bytes 75497728 | tf_op jit(solution)/shard_map/hck,fgckx->fghx/dot_general | solution.py:34
  943.3 19.4 %fusion.17 = (bf16[8,32,2,32,256,1]{4,3,2,1,0,5:T(8,128)(2,1)S(1)}, bf16[8,32,2,32,256,1]{4,3,2,1,0,5:T(8,128)(2,1)}) fusion(f32[8,32,256,2,32]{2,4,3,1,0:T(8,128)} %convolution_add_fusion.1, f32[32,2,32]{2,1,0:T(2,128)S(1)} %copy.91, f32[32,2,32]{2,1,0:T(2,128)S(1)} %copy.90, f32[8,32,256,2,32]{2,4,3,1,0:T(8,128)} %fusion.98, ...), kind=kOutput, calls=%fused_computation.49 | convolution fusion | flops 574685184 | bytes 58736896 | tf_op jit(solution)/shard_map/hck,fghx->fgckx/dot_general | solution.py:34
  973.7 14.3 fusion.29
  988.0 20.0 %convolution_subtract_fusion = f32[8,2,32,256,4,8]{3,5,4,2,1,0:T(8,128)} fusion(f32[8,2,32,256,4,8]{3,5,4,2,1,0:T(8,128)} %fusion.33, bf16[8,32,2,32,256,1]{4,3,2,1,0,5:T(8,128)(2,1)} %get-tuple-element.14, s32[4,8]{1,0:T(4,128)S(1)} %multiply_add_fusion), kind=kOutput, calls=%fused_computation.44 | convolution fusion | flops 272646144 | bytes 41943168 | tf_op jit(solution)/shard_map/gbj,fgckx->bcfjkx/dot_general | solution.py:34
  1008.0 23.1 %fusion.6 = (bf16[4,2,8,8,32,256]{5,3,0,4,1,2:T(8,128)(2,1)}, bf16[4,2,8,8,32,256]{5,3,0,4,1,2:T(8,128)(2,1)}) fusion(f32[8,2,32,256,4,8]{3,5,4,2,1,0:T(8,128)} %convolution_subtract_fusion, f32[4,2,8,8,32]{3,0,4,1,2:T(4,128)S(1)} %copy-done.6, f32[4,2,8,8,32]{3,0,4,1,2:T(4,128)S(1)} %copy-done.5, f32[8,2,32,256,4,8]{3,5,4,2,1,0:T(8,128)} %fusion.29, ...), kind=kOutput, calls=%fused_computation.16 | convolution fusion | flops 306200576 | bytes 58851456 | tf_op jit(solution)/shard_map/gbj,fgckx->bcfjkx/dot_general | solution.py:34
  1031.1 15.7 copy.98
  1046.9 15.9 copy.99
  1077.5 367.5 %all_to_all.45 = bf16[2,1,8,8,8,32,256]{6,5,4,3,1,0,2:T(8,128)(2,1)S(1)} all-to-all(bf16[2,1,8,8,8,32,256]{6,5,4,3,1,0,2:T(8,128)(2,1)} %copy.100), channel_id=1, replica_groups=mesh['aa'=4,'ba'=4,'col'=2] {'ba','col'}, dimensions={2} | all-to-all | bytes 33554432 | tf_op jit(solution)/shard_map/all_to_all | solution.py:128
  1462.5 21.2 %subtract_convert_fusion = bf16[64,8,32,256]{3,0,2,1:T(8,128)(2,1)} fusion(f32[64,8,32,256]{3,0,2,1:T(8,128)} %fusion.23, bf16[1,1,8,8,8,32,256]{6,5,4,3,1,0,2:T(8,128)(2,1)} %get-tuple-element.15), kind=kOutput, calls=%fused_computation.37 | convolution fusion | flops 545325056 | bytes 33554432 | tf_op jit(solution)/shard_map/fi,fjkx->ijkx/dot_general | solution.py:34
  1495.1 97.2 %all_to_all.46 = bf16[64,8,32,256]{3,2,1,0:T(8,128)(2,1)S(1)} all-to-all(bf16[64,8,32,256]{3,2,1,0:T(8,128)(2,1)} %copy.103), channel_id=1, replica_groups=mesh['aa'=4,'ba'=4,'col'=2] {'aa'}, dimensions={0} | all-to-all | bytes 16777216 | tf_op jit(solution)/shard_map/all_to_all | solution.py:134
  1607.4 18.7 %fusion.28 = bf16[4096,1024]{1,0:T(8,128)(2,1)} fusion(bf16[1024,1024]{1,0:T(8,128)(2,1)S(1)} %copy-done, f32[4096,1024]{1,0:T(8,128)} %bitcast.250, bf16[4096,1024]{1,0:T(8,128)(2,1)S(1)} %bitcast.246, f32[4096,3072]{1,0:T(8,128)} %fusion.236, f32[1024]{0:T(1024)S(1)} %copy-done.9), kind=kOutput, calls=%fused_computation.60 | convolution fusion | flops 8619294720 | bytes 44044288 | tf_op jit(solution)/shard_map/dot_general | solution.py:139
  (65 shorter events, 218.3 us)
Async XLA Ops:
  0.0 1607.3 %copy-start = (bf16[1024,1024]{1,0:T(8,128)(2,1)S(1)}, bf16[1024,1024]{1,0:T(8,128)(2,1)}, u32[]{:S(2)}) copy-start(bf16[1024,1024]{1,0:T(8,128)(2,1)} %param.11) | copy-start | bytes 6291460
  0.0 5.4 copy-start.7
  5.4 5.4 copy-start.8
  152.0 99.9 %all-to-all-start = ((bf16[4,2,524288]{2,1,0:T(2,128)(2,1)}), bf16[4,2,524288]{2,1,0:T(2,128)(2,1)}, u32[]{:S(2)}, u32[]{:S(2)}) async-start(bf16[4,2,524288]{2,1,0:T(2,128)(2,1)} %reshape.452), calls=%async_computation | async-start | bytes 16777216 | tf_op jit(solution)/shard_map/all_to_all | solution.py:55
  334.3 6.0 copy-start.3
  388.2 369.3 %all-to-all-start.1 = ((bf16[2,8,1,8,8,32,256]{6,5,4,3,2,0,1:T(8,128)(2,1)}), bf16[2,8,1,8,8,32,256]{6,5,4,3,2,0,1:T(8,128)(2,1)}, u32[]{:S(2)}, u32[]{:S(2)}) async-start(bf16[2,8,1,8,8,32,256]{6,5,4,3,2,0,1:T(8,128)(2,1)} %pad_maximum_fusion), calls=%async_computation.1 | async-start | bytes 33554432 | tf_op jit(solution)/shard_map/all_to_all | solution.py:71
  767.8 31.8 %copy-start.4 = (bf16[1,8,1,8,8,32,256]{6,5,4,3,2,0,1:T(8,128)(2,1)}, bf16[1,8,1,8,8,32,256]{6,5,4,3,2,0,1:T(8,128)(2,1)S(1)}, u32[]{:S(2)}) copy-start(bf16[1,8,1,8,8,32,256]{6,5,4,3,2,0,1:T(8,128)(2,1)S(1)} %get-tuple-element.18) | copy-start | bytes 25165828
  835.2 16.0 copy-start.1
  962.6 11.0 copy-start.2
  988.0 20.0 %copy-start.5 = (f32[4,2,8,8,32]{3,0,4,1,2:T(4,128)S(1)}, f32[4,2,8,8,32]{3,0,4,1,2:T(4,128)}, u32[]{:S(2)}) copy-start(f32[4,2,8,8,32]{3,0,4,1,2:T(4,128)} %copy.94) | copy-start | bytes 196612
  988.0 20.0 %copy-start.6 = (f32[4,2,8,8,32]{3,0,4,1,2:T(4,128)S(1)}, f32[4,2,8,8,32]{3,0,4,1,2:T(4,128)}, u32[]{:S(2)}) copy-start(f32[4,2,8,8,32]{3,0,4,1,2:T(4,128)} %copy.97) | copy-start | bytes 196612
  1592.3 15.1 slice-start
  1599.1 8.2 slice-start.1
  1599.1 8.2 copy-start.9
where the time goes:
time: 1630 us
  blocking collectives  465 us (29%)
  waiting for transfers between devices  451 us (28%)
  matrix products  364 us (22%)
  local copies, waits for them, and re-layouts  283 us (17%)
  other arithmetic  50.3 us (3%)
    all_to_all x1, blocking collectives, local(): lax.all_to_all(shaped, ('ba', 'col'), split_axis=2, concat_axis=1, tiled=...  368 us
    all_to_all x1, waiting for transfers between devices, local(): lax.all_to_all(shaped, ('ba', 'col'), split_axis=1, concat_axis=2, tiled=...  358 us
    dot_general x20, matrix products, contract(): return jnp.einsum(form, table, operand, preferred_element_type=jnp.float32)  314 us
    all_to_all x1, blocking collectives, local(): lax.all_to_all(conv_part, 'aa', split_axis=0, concat_axis=3, tiled=True)  97.2 us
    unnamed x27, local copies, waits for them, and re-layouts  95.7 us
    all_to_all x1, waiting for transfers between devices, local(): lax.all_to_all(local_block, 'aa', split_axis=3, concat_axis=0, tiled=True)  92.4 us
    all_to_all x1, local copies, waits for them, and re-layouts, local(): lax.all_to_all(local_block, 'aa', split_axis=3, concat_axis=0, tiled=True)  45.4 us
    reshape x1, local copies, waits for them, and re-layouts, local(): local_block = mixed.reshape(rows_i, rows_j, rows_k, D)  44.2 us
  transfers between devices with their start and end apart: 2, of which 2 were waited for; matrix products, arithmetic and copies ran while one was open for 0% of the time, Pallas kernels for 0%

commit v1 on v0

v1 whole, which is shorter than its diff:
```python
import math

import jax
import jax.numpy as jnp
from jax import lax
from jax.experimental import pallas as pl
from jax.experimental.pallas import tpu as pltpu
from jax.sharding import PartitionSpec as P

LA = 64
LB = 32
LC = 64
D = 1024


EPSILON = 1e-06


def dft_tables(length):
    counter = jnp.arange(length, dtype=jnp.int32)
    product = counter[:, None] * counter[None, :] % length
    angle = 2.0 * math.pi / length * product.astype(jnp.float32)
    factor = 1.0 / math.sqrt(length)
    return (
        (jnp.cos(angle) * factor).astype(jnp.bfloat16),
        (jnp.sin(angle) * factor).astype(jnp.bfloat16),
    )


def phase_pair(integer_phase, modulus):
    angle = 2.0 * math.pi / modulus * (integer_phase % modulus).astype(jnp.float32)
    return (jnp.cos(angle), jnp.sin(angle))


SUB = 16
CHUNKS = 2
TILE = 512
F32 = jnp.float32
BF16 = jnp.bfloat16


def params():
    return pltpu.CompilerParams(vmem_limit_bytes=56 * 1024 * 1024)


def dot(left, right):
    return jnp.dot(left, right, preferred_element_type=F32)


def with_identity(table):
    rows, cols = table.shape[-2:]
    tall = jnp.repeat(table, SUB, axis=-2)
    spread = (jnp.arange(cols)[:, None] == jnp.arange(cols * SUB)[None, :] // SUB).astype(BF16)
    wide = jnp.matmul(tall, spread, preferred_element_type=F32)
    same = jnp.arange(rows * SUB)[:, None] % SUB == jnp.arange(cols * SUB)[None, :] % SUB
    return jnp.where(same, wide, 0.0).astype(BF16)


def project(tokens, norm_gain, in_weight, parts, width):
    count, dim = tokens.shape
    sub = width // CHUNKS

    def kernel(tokens_ref, gain_ref, weight_ref, *outs):
        gate_ref = outs[-1]
        flat = tokens_ref[...].astype(F32)
        meansq = jnp.mean(flat * flat, axis=-1, keepdims=True)
        normed = (flat * lax.rsqrt(meansq + EPSILON) * gain_ref[...]).astype(BF16)
        for part in range(parts):
            at = part * width
            first = dot(normed, weight_ref[:, at : at + width])
            value = dot(normed, weight_ref[:, 2 * dim + at : 2 * dim + at + width])
            mixed = (first * value).astype(BF16)
            for chunk in range(CHUNKS):
                outs[chunk][part] = mixed[:, chunk * sub : (chunk + 1) * sub]
            gate_ref[:, at : at + width] = dot(normed, weight_ref[:, dim + at : dim + at + width]).astype(BF16)

    mixed_spec = pl.BlockSpec((parts, TILE, sub), lambda t: (0, t, 0))
    return pl.pallas_call(
        kernel,
        grid=(count // TILE,),
        in_specs=[
            pl.BlockSpec((TILE, dim), lambda t: (t, 0)),
            pl.BlockSpec((1, dim), lambda t: (0, 0)),
            pl.BlockSpec((dim, 3 * dim), lambda t: (0, 0)),
        ],
        out_specs=[mixed_spec] * CHUNKS + [pl.BlockSpec((TILE, dim), lambda t: (t, 0))],
        out_shape=[jax.ShapeDtypeStruct((parts, count, sub), BF16)] * CHUNKS
        + [jax.ShapeDtypeStruct((count, dim), BF16)],
        compiler_params=params(),
        cost_estimate=pl.CostEstimate(
            flops=6 * count * dim * dim, bytes_accessed=6 * count * dim + 6 * dim * dim, transcendentals=count
        ),
        name="project",
    )(tokens, norm_gain.reshape(1, dim), in_weight)


def finish(convs, mixes, gate, skip_gain, out_weight):
    count, dim = gate.shape
    parts, _, sub = convs[0].shape

    def kernel(*refs):
        conv_refs = refs[:CHUNKS]
        mix_refs = refs[CHUNKS : 2 * CHUNKS]
        gate_ref, skip_ref, weight_ref, out_ref = refs[2 * CHUNKS :]
        pieces = []
        for part in range(parts):
            for chunk in range(CHUNKS):
                at = (part * CHUNKS + chunk) * sub
                conv = conv_refs[chunk][part].astype(F32)
                mixed = mix_refs[chunk][part].astype(F32)
                gate_piece = gate_ref[:, at : at + sub].astype(F32)
                pieces.append((gate_piece * (conv + skip_ref[:, at : at + sub] * mixed)).astype(BF16))
        out_ref[...] = dot(jnp.concatenate(pieces, axis=1), weight_ref[...]).astype(BF16)

    chunk_spec = pl.BlockSpec((parts, TILE, sub), lambda t: (0, t, 0))
    return pl.pallas_call(
        kernel,
        grid=(count // TILE,),
        in_specs=[chunk_spec] * (2 * CHUNKS)
        + [
            pl.BlockSpec((TILE, dim), lambda t: (t, 0)),
            pl.BlockSpec((1, dim), lambda t: (0, 0)),
            pl.BlockSpec((dim, dim), lambda t: (0, 0)),
        ],
        out_specs=pl.BlockSpec((TILE, dim), lambda t: (t, 0)),
        out_shape=jax.ShapeDtypeStruct((count, dim), BF16),
        compiler_params=params(),
        cost_estimate=pl.CostEstimate(
            flops=2 * count * dim * dim, bytes_accessed=8 * count * dim + 2 * dim * dim, transcendentals=0
        ),
        name="finish",
    )(*convs, *mixes, gate, skip_gain.reshape(1, dim), out_weight)


def outer_digit(table, values, name):
    lead, rows_j, rows_k, sub = values.shape
    out_lead = table.shape[0] // SUB

    def kernel(table_ref, values_ref, out_ref):
        block = values_ref[...].reshape(lead * SUB, sub)
        out_ref[...] = dot(table_ref[...], block).astype(BF16).reshape(out_lead, 1, SUB, sub)

    return pl.pallas_call(
        kernel,
        grid=(rows_j, rows_k // SUB),
        in_specs=[
            pl.BlockSpec(table.shape, lambda j, k: (0, 0)),
            pl.BlockSpec((lead, 1, SUB, sub), lambda j, k: (0, j, k, 0)),
        ],
        out_specs=pl.BlockSpec((out_lead, 1, SUB, sub), lambda j, k: (0, j, k, 0)),
        out_shape=jax.ShapeDtypeStruct((out_lead, rows_j, rows_k, sub), BF16),
        compiler_params=params(),
        cost_estimate=pl.CostEstimate(
            flops=2 * table.shape[0] * table.shape[1] * rows_j * (rows_k // SUB) * sub,
            bytes_accessed=2 * (lead + out_lead) * rows_j * rows_k * sub,
            transcendentals=0,
        ),
        name=name,
    )(table, values)


def inner_digits(values, filters, chunk, two, two_back, three, three_back):
    count_ba, count_col, _, freq_local, rows_j, rows_k, sub = values.shape
    groups = rows_k // SUB

    def kernel(values_ref, filter_ref, two_ref, two_back_ref, three_ref, three_back_ref, out_ref, mid_ref):
        for col in range(count_col):
            for group in range(groups):
                inside = slice(group * SUB, (group + 1) * SUB)
                at = col * rows_k + group * SUB
                block = values_ref[:, col, :, 0, :, inside, :].reshape(count_ba * 2 * rows_j * SUB, sub)
                mid_ref[:, :, at : at + SUB, :] = dot(two_ref[0], block).astype(BF16).reshape(2, LB, SUB, sub)
        for index in range(LB):
            block = mid_ref[:, index].reshape(2 * LC, sub)
            spectrum = dot(three_ref[0, index], block)
            spec_real = spectrum[:LC]
            spec_imag = spectrum[LC:]
            filt_real = filter_ref[0, 0, index].astype(F32)
            filt_imag = filter_ref[1, 0, index].astype(F32)
            filtered = jnp.concatenate(
                [filt_real * spec_real - filt_imag * spec_imag, filt_real * spec_imag + filt_imag * spec_real]
            ).astype(BF16)
            mid_ref[:, index] = dot(three_back_ref[0, index], filtered).astype(BF16).reshape(2, LC, sub)
        for col in range(count_col):
            for group in range(groups):
                inside = slice(group * SUB, (group + 1) * SUB)
                at = col * rows_k + group * SUB
                block = mid_ref[:, :, at : at + SUB, :].reshape(2 * LB * SUB, sub)
                back = dot(two_back_ref[0], block).astype(BF16)
                out_ref[:, col, :, 0, :, inside, :] = back.reshape(count_ba, 2, rows_j, SUB, sub)

    shape = (count_ba, count_col, 2, 1, rows_j, rows_k, sub)
    size = 2 * LB * SUB
    moved_spec = pl.BlockSpec(shape, lambda f: (0, 0, 0, f, 0, 0, 0))
    points = freq_local * LB * LC * sub
    return pl.pallas_call(
        kernel,
        grid=(freq_local,),
        in_specs=[
            moved_spec,
            pl.BlockSpec((2, 1, LB, LC, sub), lambda f: (0, f, 0, 0, chunk)),
            pl.BlockSpec((1, size, size), lambda f: (f, 0, 0)),
            pl.BlockSpec((1, size, size), lambda f: (f, 0, 0)),
            pl.BlockSpec((1, LB, 2 * LC, 2 * LC), lambda f: (f, 0, 0, 0)),
            pl.BlockSpec((1, LB, 2 * LC, 2 * LC), lambda f: (f, 0, 0, 0)),
        ],
        out_specs=moved_spec,
        out_shape=jax.ShapeDtypeStruct(values.shape, BF16),
        scratch_shapes=[pltpu.VMEM((2, LB, LC, sub), BF16)],
        compiler_params=params(),
        cost_estimate=pl.CostEstimate(
            flops=4 * points * (2 * size + 4 * LC), bytes_accessed=12 * points, transcendentals=0
        ),
        name="inner_digits",
    )(values, filters, two, two_back, three, three_back)


def local(tokens, norm_gain, in_weight, skip_gain, spectrum_filter, out_weight):
    count_aa = lax.axis_size("aa")
    count_ba = lax.axis_size("ba")
    count_col = lax.axis_size("col")
    rows_i = LA // count_aa
    rows_j = LB // count_ba
    rows_k = LC // count_col
    blocks = count_ba * count_col
    freq_local = LA // blocks
    channels = D // count_aa
    sub = channels // CHUNKS
    points = LA * LB * LC
    count = rows_i * rows_j * rows_k

    *mixes, gate = project(tokens.reshape(count, D), norm_gain, in_weight, count_aa, channels)

    cos_a, sin_a = lax.optimization_barrier(dft_tables(LA))
    pair_a = jnp.stack([cos_a.reshape(blocks, freq_local, LA), -sin_a.reshape(blocks, freq_local, LA)], axis=1)
    pair_a = pair_a.reshape(2 * LA, LA)
    one = with_identity(pair_a)
    one_back = with_identity(pair_a.T)

    slot = lax.axis_index("ba") * count_col + lax.axis_index("col")
    freq = slot * freq_local + jnp.arange(freq_local, dtype=jnp.int32)
    index_j = jnp.arange(LB, dtype=jnp.int32)
    index_k = jnp.arange(LC, dtype=jnp.int32)
    cos_b, sin_b = (table.astype(F32)[None] for table in dft_tables(LB))
    cos_j, sin_j = phase_pair(freq[:, None] * index_j[None, :], LA * LB)
    cos_j, sin_j = cos_j[:, None, :], sin_j[:, None, :]
    real_b = cos_b * cos_j - sin_b * sin_j
    imag_b = -(cos_b * sin_j + sin_b * cos_j)
    block_b = jnp.stack([jnp.stack([real_b, -imag_b], axis=2), jnp.stack([imag_b, real_b], axis=2)], axis=1)
    block_b = block_b.reshape(freq_local, 2, LB, 2, count_ba, rows_j).transpose(0, 1, 2, 4, 3, 5)
    block_b = block_b.reshape(freq_local, 2 * LB, 2 * LB).astype(BF16)
    two = with_identity(block_b)
    two_back = with_identity(block_b.swapaxes(1, 2))

    cos_c, sin_c = (table.astype(F32)[None, None] for table in dft_tables(LC))
    whole = freq[:, None, None] + LA * index_j[None, :, None]
    cos_k, sin_k = phase_pair(whole * index_k[None, None, :], points)

    def third(cos_k, sin_k):
        real_c = cos_c * cos_k - sin_c * sin_k
        imag_c = -(cos_c * sin_k + sin_c * cos_k)
        return real_c, imag_c

    def joined(a, b, c, d):
        return jnp.concatenate([jnp.concatenate([a, b], axis=-1), jnp.concatenate([c, d], axis=-1)], axis=-2).astype(BF16)

    real_c, imag_c = third(cos_k[:, :, None, :], sin_k[:, :, None, :])
    three = joined(real_c, -imag_c, imag_c, real_c)
    real_t, imag_t = third(cos_k[:, :, :, None], sin_k[:, :, :, None])
    three_back = joined(real_t, imag_t, -imag_t, real_t)

    rows = [lax.all_to_all(mixed, "aa", split_axis=0, concat_axis=0, tiled=True) for mixed in mixes]
    moved = []
    for chunk in range(CHUNKS):
        first = outer_digit(one, rows[chunk].reshape(LA, rows_j, rows_k, sub), "first_digit")
        first = first.reshape(blocks, 2, freq_local, rows_j, rows_k, sub)
        moved.append(lax.all_to_all(first, ("ba", "col"), split_axis=0, concat_axis=0, tiled=True))
    returned = []
    for chunk in range(CHUNKS):
        values = moved[chunk].reshape(count_ba, count_col, 2, freq_local, rows_j, rows_k, sub)
        back = inner_digits(values, spectrum_filter, chunk, two, two_back, three, three_back)
        back = back.reshape(blocks, 2, freq_local, rows_j, rows_k, sub)
        returned.append(lax.all_to_all(back, ("ba", "col"), split_axis=0, concat_axis=0, tiled=True))
    convs = []
    for chunk in range(CHUNKS):
        conv = outer_digit(one_back, returned[chunk].reshape(2 * LA, rows_j, rows_k, sub), "last_digit")
        conv = conv.reshape(count_aa, count, sub)
        convs.append(lax.all_to_all(conv, "aa", split_axis=0, concat_axis=0, tiled=True))
    layer_out = finish(convs, mixes, gate, skip_gain, out_weight)
    return layer_out.reshape(rows_i, rows_j, rows_k, D)


def solution(mesh):
    in_specs = (
        P("aa", "ba", "col", None),
        P(),
        P(),
        P(),
        P(None, ("ba", "col"), None, None, "aa"),
        P(),
    )
    out_specs = P("aa", "ba", "col", None)
    return jax.shard_map(local, mesh=mesh, in_specs=in_specs, out_specs=out_specs, check_vma=False)
```

time: 1630 us -> 1020 us (0.63)
  blocking collectives: 465 us -> 108 us
  matrix products: 364 us -> 22.4 us
  local copies, waits for them, and re-layouts: 283 us -> 1.01 us
  Pallas kernels: 0 us -> 239 us
  waiting for transfers between devices: 451 us -> 585 us
  other arithmetic: 50.3 us -> 29.7 us
  starting transfers between devices: 12.7 us -> 31.6 us
    all_to_all x2, blocking collectives: 465 us -> 108 us  [the longest x1 54.5 us: local(): lax.all_to_all(mixed, 'aa', split_axis=0, concat_axis=0, tiled=True)]
    dot_general x22 -> x4, matrix products: 364 us -> 22.4 us  [with_identity(): wide = jnp.matmul(tall, spread, preferred_element_type=F32)]
    pallas_call x0 -> x8, Pallas kernels: none -> 239 us  [the longest x4 94.6 us: outer_digit(): pl.pallas_call(kernel, grid=(rows_j, rows_k // SUB), in_specs=[pl.BlockSp...]
    all_to_all x2 -> x6, waiting for transfers between devices: 451 us -> 585 us  [the longest x2 291 us: local(): lax.all_to_all(back, ('ba', 'col'), split_axis=0, concat_axis=0, tiled=True)]
    unnamed x27 -> x0, local copies, waits for them, and re-layouts: 95.7 us -> none
    another operation x5 -> x0, local copies, waits for them, and re-layouts: 61.2 us -> none
    all_to_all x1 -> x0, local copies, waits for them, and re-layouts: 45.4 us -> none  [local(): lax.all_to_all(local_block, 'aa', split_axis=3, concat_axis=0, tiled=True)]
    reshape x1 -> x0, local copies, waits for them, and re-layouts: 44.2 us -> none  [local(): local_block = mixed.reshape(rows_i, rows_j, rows_k, D)]
  transfers between devices with their start and end apart: 2 -> 6, of which waited for: 2 -> 6; matrix products, arithmetic and copies ran while one was open for 0% -> 5% of each run, Pallas kernels for 0% -> 18%
where the time goes in v1:
time: 1020 us
  waiting for transfers between devices  585 us (57%)
  Pallas kernels  239 us (23%)
  blocking collectives  108 us (11%)
  starting transfers between devices  31.6 us (3%)
  other arithmetic  29.7 us (3%)
  matrix products  22.4 us (2%)
    all_to_all x2, waiting for transfers between devices, local(): lax.all_to_all(back, ('ba', 'col'), split_axis=0, concat_axis=0, tiled=True)  291 us
    all_to_all x2, waiting for transfers between devices, local(): lax.all_to_all(first, ('ba', 'col'), split_axis=0, concat_axis=0, tiled=T...  248 us
    pallas_call x4, Pallas kernels, outer_digit(): pl.pallas_call(kernel, grid=(rows_j, rows_k // SUB), in_specs=[pl.BlockSp...  94.6 us
    pallas_call x2, Pallas kernels, inner_digits(): pl.pallas_call(kernel, grid=(freq_local,), in_specs=[moved_spec, pl.Block...  93.1 us
    all_to_all x1, blocking collectives, local(): lax.all_to_all(mixed, 'aa', split_axis=0, concat_axis=0, tiled=True)  54.5 us
    all_to_all x1, blocking collectives, local(): lax.all_to_all(conv, 'aa', split_axis=0, concat_axis=0, tiled=True)  53.8 us
    pallas_call x1, Pallas kernels, project(): pl.pallas_call(kernel, grid=(count // TILE,), in_specs=[pl.BlockSpec((TIL...  33.7 us
    all_to_all x1, waiting for transfers between devices, local(): lax.all_to_all(conv, 'aa', split_axis=0, concat_axis=0, tiled=True)  24.7 us
  transfers between devices with their start and end apart: 6, of which 6 were waited for; matrix products, arithmetic and copies ran while one was open for 5% of the time, Pallas kernels for 18%

profile of v1, /device:TPU:0, one launch (start us, length us, event | category | flops | bytes accessed | tf_op | source)
XLA Modules:
  0.0 1016.5 jit_solution(6672598302012979938)
XLA Ops:
  0.0 33.7 %project.1 = (bf16[4,4096,128]{2,1,0:T(8,128)(2,1)}, bf16[4,4096,128]{2,1,0:T(8,128)(2,1)}, bf16[4096,1024]{1,0:T(8,128)(2,1)}) custom-call(bf16[4096,1024]{1,0:T(8,128)(2,1)} %bitcast.55, f32[1,1024]{1,0:T(1,128)} %bitcast.56, bf16[1024,3072]{1,0:T(8,128)(2,1)} %weight_ref.1), custom_call_target="tpu_custom_call" | custom-call | flops 25769803776 | bytes 31457280 | tf_op jit(solution)/shard_map/project/pallas_call | solution.py:78
  33.7 54.5 %all_to_all.40 = bf16[4,4096,128]{2,1,0:T(8,128)(2,1)} all-to-all(bf16[4,4096,128]{2,1,0:T(8,128)(2,1)} %get-tuple-element.13.refs_3_), channel_id=1, replica_groups=mesh['aa'=4,'ba'=4,'col'=2] {'aa'}, dimensions={0} | all-to-all | bytes 8388608 | tf_op jit(solution)/shard_map/all_to_all | solution.py:272
  96.1 23.8 %first_digit.3 = bf16[128,8,32,128]{3,2,1,0:T(8,128)(2,1)} custom-call(bf16[2048,1024]{1,0:T(8,128)(2,1)} %select_convert_fusion.2.table_ref, bf16[64,8,32,128]{3,2,1,0:T(8,128)(2,1)} %bitcast.43), custom_call_target="tpu_custom_call" | custom-call | flops 8589934592 | bytes 12582912 | tf_op jit(solution)/shard_map/first_digit/pallas_call | solution.py:143
  119.9 21.4 %all-to-all-done = bf16[4,4096,128]{2,1,0:T(8,128)(2,1)} async-done(((bf16[4,4096,128]{2,1,0:T(8,128)(2,1)}), bf16[4,4096,128]{2,1,0:T(8,128)(2,1)}, u32[]{:S(2)}, u32[]{:S(2)}) %all-to-all-start) | async-done | bytes 4194336 | tf_op jit(solution)/shard_map/all_to_all | solution.py:272
  141.3 6.7 all-to-all-start.5
  148.0 23.7 %first_digit.2 = bf16[128,8,32,128]{3,2,1,0:T(8,128)(2,1)} custom-call(bf16[2048,1024]{1,0:T(8,128)(2,1)} %select_convert_fusion.2.table_ref, bf16[64,8,32,128]{3,2,1,0:T(8,128)(2,1)} %bitcast.8.values_ref), custom_call_target="tpu_custom_call" | custom-call | flops 8589934592 | bytes 12582912 | tf_op jit(solution)/shard_map/first_digit/pallas_call | solution.py:143
  171.7 159.2 %all-to-all-done.5 = bf16[8,2,8,8,32,128]{5,4,3,2,1,0:T(8,128)(2,1)} async-done(((bf16[8,2,8,8,32,128]{5,4,3,2,1,0:T(8,128)(2,1)}), bf16[8,2,8,8,32,128]{5,4,3,2,1,0:T(8,128)(2,1)}, u32[]{:S(2)}, u32[]{:S(2)}) %all-to-all-start.5) | async-done | bytes 8388640 | tf_op jit(solution)/shard_map/all_to_all | solution.py:277
  330.8 5.2 all-to-all-start.1
  340.1 8.2 select_convert_fusion.1.two_ref
  348.6 8.2 select_convert_fusion.two_back_ref
  356.8 8.9 negate_convert_fusion
  365.7 17.1 %maximum_maximum_fusion = (bf16[8,32,128,128]{3,2,1,0:T(8,128)(2,1)}, bf16[8,32,128,128]{3,2,1,0:T(8,128)(2,1)}) fusion(bf16[8,32,64,64]{3,2,1,0:T(8,128)(2,1)} %get-tuple-element.20, bf16[8,32,64,64]{3,2,1,0:T(8,128)(2,1)S(1)} %get-tuple-element.17, bf16[8,32,64,64]{3,2,1,0:T(8,128)(2,1)S(1)} %get-tuple-element.16, ...), kind=kLoop, calls=%fused_computation.2 | loop fusion | flops 67108864 | bytes 29360128 | tf_op jit(solution)/shard_map/concatenate | solution.py:265
  382.9 46.6 %inner_digits.3 = bf16[4,2,2,8,8,32,128]{6,5,4,3,2,1,0:T(8,128)(2,1)} custom-call(bf16[4,2,2,8,8,32,128]{6,5,4,3,2,1,0:T(8,128)(2,1)} %bitcast.21.values_ref, bf16[2,8,32,64,256]{4,3,2,1,0:T(8,128)(2,1)} %filter_ref.3, bf16[8,1024,1024]{2,1,0:T(8,128)(2,1)} %select_convert_fusion.1.two_ref, bf16[8,1024,1024]{2,1,0:T(8,128)(2,1)} %select_convert_fusion.two_back_ref, ...), custom_call_target="tpu_custom_call" | custom-call | flops 19327352832 | bytes 25165824 | tf_op jit(solution)/shard_map/inner_digits/pallas_call | solution.py:196
  429.4 88.4 %all-to-all-done.1 = bf16[8,2,8,8,32,128]{5,4,3,2,1,0:T(8,128)(2,1)} async-done(((bf16[8,2,8,8,32,128]{5,4,3,2,1,0:T(8,128)(2,1)}), bf16[8,2,8,8,32,128]{5,4,3,2,1,0:T(8,128)(2,1)}, u32[]{:S(2)}, u32[]{:S(2)}) %all-to-all-start.1) | async-done | bytes 8388640 | tf_op jit(solution)/shard_map/all_to_all | solution.py:277
  517.8 5.0 all-to-all-start.6
  522.8 46.6 %inner_digits.2 = bf16[4,2,2,8,8,32,128]{6,5,4,3,2,1,0:T(8,128)(2,1)} custom-call(bf16[4,2,2,8,8,32,128]{6,5,4,3,2,1,0:T(8,128)(2,1)} %bitcast.10.values_ref, bf16[2,8,32,64,256]{4,3,2,1,0:T(8,128)(2,1)} %filter_ref.3, bf16[8,1024,1024]{2,1,0:T(8,128)(2,1)} %select_convert_fusion.1.two_ref, bf16[8,1024,1024]{2,1,0:T(8,128)(2,1)} %select_convert_fusion.two_back_ref, ...), custom_call_target="tpu_custom_call" | custom-call | flops 19327352832 | bytes 25165824 | tf_op jit(solution)/shard_map/inner_digits/pallas_call | solution.py:196
  569.4 135.8 %all-to-all-done.6 = bf16[8,2,8,8,32,128]{5,4,3,2,1,0:T(8,128)(2,1)} async-done(((bf16[8,2,8,8,32,128]{5,4,3,2,1,0:T(8,128)(2,1)}), bf16[8,2,8,8,32,128]{5,4,3,2,1,0:T(8,128)(2,1)}, u32[]{:S(2)}, u32[]{:S(2)}) %all-to-all-start.6) | async-done | bytes 8388640 | tf_op jit(solution)/shard_map/all_to_all | solution.py:283
  705.1 5.0 all-to-all-start.2
  713.5 23.6 %last_digit.3 = bf16[64,8,32,128]{3,2,1,0:T(8,128)(2,1)} custom-call(bf16[1024,2048]{1,0:T(8,128)(2,1)} %select_convert_fusion.3.table_ref, bf16[128,8,32,128]{3,2,1,0:T(8,128)(2,1)} %bitcast.23.values_ref), custom_call_target="tpu_custom_call" | custom-call | flops 8589934592 | bytes 12582912 | tf_op jit(solution)/shard_map/last_digit/pallas_call | solution.py:143
  737.0 155.3 %all-to-all-done.2 = bf16[8,2,8,8,32,128]{5,4,3,2,1,0:T(8,128)(2,1)} async-done(((bf16[8,2,8,8,32,128]{5,4,3,2,1,0:T(8,128)(2,1)}), bf16[8,2,8,8,32,128]{5,4,3,2,1,0:T(8,128)(2,1)}, u32[]{:S(2)}, u32[]{:S(2)}) %all-to-all-start.2) | async-done | bytes 8388640 | tf_op jit(solution)/shard_map/all_to_all | solution.py:283
  897.3 23.5 %last_digit.2 = bf16[64,8,32,128]{3,2,1,0:T(8,128)(2,1)} custom-call(bf16[1024,2048]{1,0:T(8,128)(2,1)} %select_convert_fusion.3.table_ref, bf16[128,8,32,128]{3,2,1,0:T(8,128)(2,1)} %bitcast.17.values_ref), custom_call_target="tpu_custom_call" | custom-call | flops 8589934592 | bytes 12582912 | tf_op jit(solution)/shard_map/last_digit/pallas_call | solution.py:143
  920.8 24.7 %all-to-all-done.7.refs_1_ = bf16[4,4096,128]{2,1,0:T(8,128)(2,1)} async-done(((bf16[4,4096,128]{2,1,0:T(8,128)(2,1)}), bf16[4,4096,128]{2,1,0:T(8,128)(2,1)}, u32[]{:S(2)}, u32[]{:S(2)}) %all-to-all-start.7) | async-done | bytes 4194336 | tf_op jit(solution)/shard_map/all_to_all | solution.py:288
  945.5 53.8 %all_to_all.41.refs_0_ = bf16[4,4096,128]{2,1,0:T(8,128)(2,1)} all-to-all(bf16[4,4096,128]{2,1,0:T(8,128)(2,1)} %bitcast.45), channel_id=1, replica_groups=mesh['aa'=4,'ba'=4,'col'=2] {'aa'}, dimensions={0} | all-to-all | bytes 8388608 | tf_op jit(solution)/shard_map/all_to_all | solution.py:288
  999.3 17.3 %finish.1 = bf16[4096,1024]{1,0:T(8,128)(2,1)} custom-call(bf16[4,4096,128]{2,1,0:T(8,128)(2,1)} %all_to_all.41.refs_0_, bf16[4,4096,128]{2,1,0:T(8,128)(2,1)} %all-to-all-done.7.refs_1_, bf16[4,4096,128]{2,1,0:T(8,128)(2,1)} %get-tuple-element.12.refs_2_, bf16[4,4096,128]{2,1,0:T(8,128)(2,1)} %get-tuple-element.13.refs_3_, ...), custom_call_target="tpu_custom_call" | custom-call | flops 8589934592 | bytes 35651584 | tf_op jit(solution)/shard_map/finish/pallas_call | solution.py:116
  (29 shorter events, 20.5 us)
Async XLA Ops:
  88.1 53.2 %all-to-all-start = ((bf16[4,4096,128]{2,1,0:T(8,128)(2,1)}), bf16[4,4096,128]{2,1,0:T(8,128)(2,1)}, u32[]{:S(2)}, u32[]{:S(2)}) async-start(bf16[4,4096,128]{2,1,0:T(8,128)(2,1)} %get-tuple-element.12.refs_2_), calls=%async_computation | async-start | bytes 8388608 | tf_op jit(solution)/shard_map/all_to_all | solution.py:272
  141.3 189.5 %all-to-all-start.5 = ((bf16[8,2,8,8,32,128]{5,4,3,2,1,0:T(8,128)(2,1)}), bf16[8,2,8,8,32,128]{5,4,3,2,1,0:T(8,128)(2,1)}, u32[]{:S(2)}, u32[]{:S(2)}) async-start(bf16[8,2,8,8,32,128]{5,4,3,2,1,0:T(8,128)(2,1)} %bitcast.42), calls=%async_computation.5 | async-start | bytes 16777216 | tf_op jit(solution)/shard_map/all_to_all | solution.py:277
  330.8 187.0 %all-to-all-start.1 = ((bf16[8,2,8,8,32,128]{5,4,3,2,1,0:T(8,128)(2,1)}), bf16[8,2,8,8,32,128]{5,4,3,2,1,0:T(8,128)(2,1)}, u32[]{:S(2)}, u32[]{:S(2)}) async-start(bf16[8,2,8,8,32,128]{5,4,3,2,1,0:T(8,128)(2,1)} %bitcast.41), calls=%async_computation.1 | async-start | bytes 16777216 | tf_op jit(solution)/shard_map/all_to_all | solution.py:277
  517.8 187.3 %all-to-all-start.6 = ((bf16[8,2,8,8,32,128]{5,4,3,2,1,0:T(8,128)(2,1)}), bf16[8,2,8,8,32,128]{5,4,3,2,1,0:T(8,128)(2,1)}, u32[]{:S(2)}, u32[]{:S(2)}) async-start(bf16[8,2,8,8,32,128]{5,4,3,2,1,0:T(8,128)(2,1)} %bitcast.40), calls=%async_computation.6 | async-start | bytes 16777216 | tf_op jit(solution)/shard_map/all_to_all | solution.py:283
  705.1 187.2 %all-to-all-start.2 = ((bf16[8,2,8,8,32,128]{5,4,3,2,1,0:T(8,128)(2,1)}), bf16[8,2,8,8,32,128]{5,4,3,2,1,0:T(8,128)(2,1)}, u32[]{:S(2)}, u32[]{:S(2)}) async-start(bf16[8,2,8,8,32,128]{5,4,3,2,1,0:T(8,128)(2,1)} %bitcast.39), calls=%async_computation.2 | async-start | bytes 16777216 | tf_op jit(solution)/shard_map/all_to_all | solution.py:283
  892.3 53.2 %all-to-all-start.7 = ((bf16[4,4096,128]{2,1,0:T(8,128)(2,1)}), bf16[4,4096,128]{2,1,0:T(8,128)(2,1)}, u32[]{:S(2)}, u32[]{:S(2)}) async-start(bf16[4,4096,128]{2,1,0:T(8,128)(2,1)} %bitcast.44), calls=%async_computation.7 | async-start | bytes 8388608 | tf_op jit(solution)/shard_map/all_to_all | solution.py:288
